TPU v7x, 32 devices: a whole 2x2x4 slice. The times are simulated.
32 devices in a mesh: rep: 2 (over x), blk: 16 (over z, y, core).
Axes of the slice: x: 2, y: 2, z: 4, core: 2. Of those that a mesh axis runs over, the one named last changes fastest.
Arguments:
- positions: float32 [3, 8192], P(None, ('rep', 'blk')), parts along dimension 1, may hold values from 0 to 64
- forces: float32 [6, 3, 8192], P(None, None, ('rep', 'blk')), parts along dimension 2, may hold values from -6 to 6
- random_kicks: float32 [6, 3, 8192], P(None, None, ('rep', 'blk')), parts along dimension 2, may hold values from -4 to 4
- history_velocity: float32 [128, 3, 8192], P(None, None, ('rep', 'blk')), parts along dimension 2, may hold values from -6 to 6
- history_offset: float32 [128, 3, 8192], P(None, None, ('rep', 'blk')), parts along dimension 2, may hold values from -8 to 8
- lag_index: int32 [4096], P(('rep', 'blk')), parts along dimension 0, may hold values from 0 to 127
Outputs:
- final_positions: float32 [3, 8192], P(None, ('rep', 'blk')), parts along dimension 1
- velocity: float32 [3, 8192], P(None, ('rep', 'blk')), parts along dimension 1
- statistics: float32 [2, 4096], P(None, ('rep', 'blk')), parts along dimension 1
There are 2 independent parts, one for each index of `rep`. A program takes and returns all parts, laid end to end along the dimension named above; each array names one. Nothing has to cross between parts.
All inputs are finite; a program needn't handle non-finite values.
Results may differ from a plain program's by a relative error of at most 0.0003.
Values sent between devices are 32-bit elements; how exact they have to be, the bound alone decides.
A program may use at most 64 MiB of HBM per device.

v0:
```python
import math
import jax
import jax.numpy as jnp
from jax import lax
from jax.sharding import PartitionSpec as P

STEPS = 6
time_step = 0.05


def pair_coefs(targets, sources):
    separation = targets[:, None, :] - sources[:, :, None]
    dist_sq = jnp.sum(separation * separation, axis=0)
    dist_safe = jnp.where(dist_sq > 0.0, dist_sq, 1.0)
    inv_dist = lax.rsqrt(dist_safe)
    distance = dist_sq * inv_dist
    inv_sq = 1.0 / dist_safe
    far_mask = distance >= 2.0
    coef_iso = jnp.where(
        far_mask, 0.75 * inv_dist * (1.0 + 2.0 / 3.0 * inv_sq), 1.0 - 9.0 / 32.0 * distance
    )
    coef_dir = jnp.where(
        far_mask, 0.75 * inv_dist * (1.0 - 2.0 * inv_sq) * inv_sq, 3.0 / 32.0 * inv_dist
    )
    return (separation, coef_iso, coef_dir)


def pair_velocity(targets, sources, loads):
    separation, coef_iso, coef_dir = pair_coefs(targets, sources)
    projection = jnp.sum(separation * loads[:, :, None], axis=0)
    return jnp.sum(
        coef_iso[None] * loads[:, :, None] + (coef_dir * projection)[None] * separation, axis=1
    )


def blockwise(targets, sources, loads):
    source_count = sources.shape[1]
    row_count = math.gcd(source_count, 512)
    block_count = source_count // row_count
    source_blocks = sources.reshape(3, block_count, row_count).transpose(1, 0, 2)
    load_blocks = loads.reshape(3, block_count, row_count).transpose(1, 0, 2)

    def accumulate(running, source_block):
        return (running + pair_velocity(targets, source_block[0], source_block[1]), None)

    running, unused = lax.scan(
        accumulate, jnp.zeros(targets.shape, jnp.float32), (source_blocks, load_blocks)
    )
    return running


def local(positions, forces, random_kicks, history_velocity, history_offset, lag_index):
    places = positions
    velocity = jnp.zeros_like(positions)
    all_forces = lax.all_gather(forces, "blk", axis=2, tiled=True)
    for step_index in range(STEPS):
        targets = places
        step_forces = all_forces[step_index]
        velocity = blockwise(
            targets, lax.all_gather(targets, "blk", axis=1, tiled=True), step_forces
        )
        places = places + time_step * velocity + random_kicks[step_index]
    velocity_dot = jnp.sum(velocity[None] * history_velocity, axis=(1, 2))
    moved = places[None] - positions[None] - history_offset
    square_disp = jnp.sum(moved * moved, axis=(1, 2))
    frames = history_velocity.shape[0]
    sphere_total = jnp.float32(positions.shape[1] * lax.axis_size("blk"))
    every_lag = lax.all_gather(lag_index, "blk", axis=0, tiled=True)
    onehot = (every_lag[:, None] == jnp.arange(frames, dtype=jnp.int32)[None, :]).astype(
        jnp.float32
    )
    frame_table = jnp.stack([velocity_dot, square_disp], axis=0)
    local_terms = jnp.dot(
        frame_table, onehot.T, precision=lax.Precision.HIGHEST, preferred_element_type=jnp.float32
    )
    statistics = (
        lax.psum_scatter(local_terms, "blk", scatter_dimension=1, tiled=True) / sphere_total
    )
    return (places, velocity, statistics)


def solution(mesh):
    return jax.shard_map(
        local,
        mesh=mesh,
        in_specs=(
            P(None, ("rep", "blk")),
            P(None, None, ("rep", "blk")),
            P(None, None, ("rep", "blk")),
            P(None, None, ("rep", "blk")),
            P(None, None, ("rep", "blk")),
            P(("rep", "blk")),
        ),
        out_specs=(P(None, ("rep", "blk")), P(None, ("rep", "blk")), P(None, ("rep", "blk"))),
        check_vma=False,
    )
```

profile of v0, /device:TPU:0, one launch (start us, length us, event | category | flops | bytes accessed | tf_op | source)
XLA Modules:
  0.0 293.1 jit_solution(7134342505187755510)
XLA Ops:
  7.3 24.4 %all_gather.25 = f32[6,3,4096]{2,1,0:T(4,128)S(1)} all-gather(f32[6,3,256]{2,1,0:T(4,128)} %param.19), channel_id=1, replica_groups=mesh['rep'=2,'blk'=16] {'blk'}, dimensions={2}, use_global_device_ids=true | all-gather | bytes 313344 | tf_op jit(solution)/shard_map/all_gather | solution.py:55
  31.8 17.6 %all_gather.24 = f32[3,4096]{1,0:T(4,128)S(1)} all-gather(f32[3,256]{1,0:T(4,128)S(1)} %copy-done), channel_id=1, replica_groups=mesh['rep'=2,'blk'=16] {'blk'}, dimensions={1}, use_global_device_ids=true | all-gather | bytes 52224 | tf_op jit(solution)/shard_map/all_gather | solution.py:60
  49.4 11.2 %while.66 = (s32[]{:T(128)}, f32[3,256]{1,0:T(4,128)S(1)}, f32[3,256]{1,0:T(4,128)S(1)}, f32[8,3,512]{2,1,0:T(4,128)S(1)}, f32[8,3,512]{2,1,0:T(4,128)S(1)}, /*index=5*/s32[]{:T(128)}, s32[]{:T(128)}) while((s32[]{:T(128)}, f32[3,256]{1,0:T(4,128)S(1)}, f32[3,256]{1,0:T(4,128)S(1)}, f32[8,3,512]{2,1,0:T(4,128)S(1)}, ...), condition=%wide.region_4.5_spmd.clone, body=%wide.region_0.4_spmd.clone.sunk | while | flops 6161155 | bytes 4261979 | solution.py:46
  50.3 0.5 fusion.68
  51.7 0.5 fusion.68
  53.1 0.5 fusion.68
  54.5 0.5 fusion.68
  55.9 0.5 fusion.68
  57.3 0.5 fusion.68
  58.7 0.5 fusion.68
  60.1 0.5 fusion.68
  60.6 18.9 %all_gather.26 = f32[3,4096]{1,0:T(4,128)S(1)} all-gather(f32[3,256]{1,0:T(4,128)S(1)} %bitcast_add_fusion.5), channel_id=1, replica_groups=mesh['rep'=2,'blk'=16] {'blk'}, dimensions={1}, use_global_device_ids=true | all-gather | bytes 52224 | tf_op jit(solution)/shard_map/all_gather | solution.py:60
  79.5 11.2 %while.67 = (s32[]{:T(128)}, f32[3,256]{1,0:T(4,128)S(1)}, f32[3,256]{1,0:T(4,128)S(1)}, f32[8,3,512]{2,1,0:T(4,128)S(1)}, f32[8,3,512]{2,1,0:T(4,128)S(1)}, /*index=5*/s32[]{:T(128)}, s32[]{:T(128)}) while((s32[]{:T(128)}, f32[3,256]{1,0:T(4,128)S(1)}, f32[3,256]{1,0:T(4,128)S(1)}, f32[8,3,512]{2,1,0:T(4,128)S(1)}, ...), condition=%wide.region_9.10_spmd.clone, body=%wide.region_5.9_spmd.clone.sunk | while | flops 6161155 | bytes 4261979 | solution.py:46
  80.4 0.5 fusion.70
  81.8 0.5 fusion.70
  83.2 0.5 fusion.70
  84.6 0.5 fusion.70
  86.0 0.5 fusion.70
  90.7 17.6 %all_gather.27 = f32[3,4096]{1,0:T(4,128)S(1)} all-gather(f32[3,256]{1,0:T(4,128)S(1)} %bitcast_add_fusion.4), channel_id=1, replica_groups=mesh['rep'=2,'blk'=16] {'blk'}, dimensions={1}, use_global_device_ids=true | all-gather | bytes 52224 | tf_op jit(solution)/shard_map/all_gather | solution.py:60
  108.3 11.2 %while.68 = (s32[]{:T(128)}, f32[3,256]{1,0:T(4,128)S(1)}, f32[3,256]{1,0:T(4,128)S(1)}, f32[8,3,512]{2,1,0:T(4,128)S(1)}, f32[8,3,512]{2,1,0:T(4,128)S(1)}, /*index=5*/s32[]{:T(128)}, s32[]{:T(128)}) while((s32[]{:T(128)}, f32[3,256]{1,0:T(4,128)S(1)}, f32[3,256]{1,0:T(4,128)S(1)}, f32[8,3,512]{2,1,0:T(4,128)S(1)}, ...), condition=%wide.region_14.15_spmd.clone, body=%wide.region_10.14_spmd.clone.sunk | while | flops 6161155 | bytes 4261979 | solution.py:46
  119.5 18.9 %all_gather.28 = f32[3,4096]{1,0:T(4,128)S(1)} all-gather(f32[3,256]{1,0:T(4,128)S(1)} %bitcast_add_fusion.3), channel_id=1, replica_groups=mesh['rep'=2,'blk'=16] {'blk'}, dimensions={1}, use_global_device_ids=true | all-gather | bytes 52224 | tf_op jit(solution)/shard_map/all_gather | solution.py:60
  138.5 11.2 %while.69 = (s32[]{:T(128)}, f32[3,256]{1,0:T(4,128)S(1)}, f32[3,256]{1,0:T(4,128)S(1)}, f32[8,3,512]{2,1,0:T(4,128)S(1)}, f32[8,3,512]{2,1,0:T(4,128)S(1)}, /*index=5*/s32[]{:T(128)}, s32[]{:T(128)}) while((s32[]{:T(128)}, f32[3,256]{1,0:T(4,128)S(1)}, f32[3,256]{1,0:T(4,128)S(1)}, f32[8,3,512]{2,1,0:T(4,128)S(1)}, ...), condition=%wide.region_19.20_spmd.clone, body=%wide.region_15.19_spmd.clone.sunk | while | flops 6161155 | bytes 4261979 | solution.py:46
  149.6 17.6 %all_gather.29 = f32[3,4096]{1,0:T(4,128)S(1)} all-gather(f32[3,256]{1,0:T(4,128)S(1)} %bitcast_add_fusion.2), channel_id=1, replica_groups=mesh['rep'=2,'blk'=16] {'blk'}, dimensions={1}, use_global_device_ids=true | all-gather | bytes 52224 | tf_op jit(solution)/shard_map/all_gather | solution.py:60
  167.3 11.1 %while.70 = (s32[]{:T(128)}, f32[3,256]{1,0:T(4,128)S(1)}, f32[3,256]{1,0:T(4,128)S(1)}, f32[8,3,512]{2,1,0:T(4,128)S(1)}, f32[8,3,512]{2,1,0:T(4,128)S(1)}, /*index=5*/s32[]{:T(128)}, s32[]{:T(128)}) while((s32[]{:T(128)}, f32[3,256]{1,0:T(4,128)S(1)}, f32[3,256]{1,0:T(4,128)S(1)}, f32[8,3,512]{2,1,0:T(4,128)S(1)}, ...), condition=%wide.region_24.25_spmd.clone, body=%wide.region_20.24_spmd.clone.sunk | while | flops 6161155 | bytes 4261979 | solution.py:46
  178.4 18.9 %all_gather.30 = f32[3,4096]{1,0:T(4,128)S(1)} all-gather(f32[3,256]{1,0:T(4,128)S(1)} %bitcast_add_fusion.1), channel_id=1, replica_groups=mesh['rep'=2,'blk'=16] {'blk'}, dimensions={1}, use_global_device_ids=true | all-gather | bytes 52224 | tf_op jit(solution)/shard_map/all_gather | solution.py:60
  197.4 11.2 %while.71 = (s32[]{:T(128)}, f32[3,256]{1,0:T(4,128)S(1)}, f32[3,256]{1,0:T(4,128)S(1)}, f32[8,3,512]{2,1,0:T(4,128)S(1)}, f32[8,3,512]{2,1,0:T(4,128)S(1)}, /*index=5*/s32[]{:T(128)}, s32[]{:T(128)}) while((s32[]{:T(128)}, f32[3,256]{1,0:T(4,128)S(1)}, f32[3,256]{1,0:T(4,128)S(1)}, f32[8,3,512]{2,1,0:T(4,128)S(1)}, ...), condition=%wide.region_29.30_spmd.clone, body=%wide.region_25.29_spmd.clone.sunk | while | flops 6161155 | bytes 4261979 | solution.py:46
  208.5 0.6 fusion.53
  209.3 17.5 %all-gather = s32[16,1,128]{2,1,0:T(1,128)S(1)} all-gather(s32[1,1,128]{2,1,0:T(1,128)S(1)} %bitcast.108), channel_id=1, replica_groups=mesh['rep'=2,'blk'=16] {'blk'}, dimensions={0}, use_global_device_ids=true | all-gather | bytes 8704 | tf_op jit(solution)/shard_map/all_gather | solution.py:68
  226.8 1.7 convolution_bitcast_fusion
  228.6 56.2 %reduce-scatter.4.cloned.1.call-done = f32[128,2]{1,0:T(8,128)} async-done(((f32[2048,2]{1,0:T(8,128)}), f32[128,2]{1,0:T(8,128)}) %reduce-scatter.4.cloned.1.call-update) | async-done | bytes 1040
  284.8 0.9 copy.25
  285.7 0.6 broadcast_multiply_fusion
  (255 shorter events, 58.8 us)
Async XLA Ops:
  7.2 24.6 %copy-start = (f32[3,256]{1,0:T(4,128)S(1)}, f32[3,256]{1,0:T(4,128)}, u32[]{:S(2)}) copy-start(f32[3,256]{1,0:T(4,128)} %param.18) | copy-start | bytes 9220
  7.2 277.6 %reduce-scatter.4.cloned.1.call-start = ((), (), s32[]{:S(2)}) async-start(), calls=%async_computation.1 | async-start | bytes 1114112
  49.4 11.2 %copy-start.4 = (f32[6,3,256]{2,1,0:T(4,128)S(1)}, f32[6,3,256]{2,1,0:T(4,128)}, u32[]{:S(2)}) copy-start(f32[6,3,256]{2,1,0:T(4,128)} %param.20) | copy-start | bytes 55300
  197.3 11.8 %copy-start.1 = (f32[128,3,256]{2,0,1:T(8,128)S(1)}, f32[128,3,256]{2,0,1:T(8,128)}, u32[]{:S(2)}) copy-start(f32[128,3,256]{2,0,1:T(8,128)} %param.21) | copy-start | bytes 1179652
  197.3 11.9 %copy-start.5 = (s32[128]{0:T(128)S(1)}, s32[128]{0:T(128)}, u32[]{:S(2)}) copy-start(s32[128]{0:T(128)} %param.23) | copy-start | bytes 1540
  197.3 29.4 %copy-start.2 = (f32[128,3,256]{2,0,1:T(8,128)S(1)}, f32[128,3,256]{2,0,1:T(8,128)}, u32[]{:S(2)}) copy-start(f32[128,3,256]{2,0,1:T(8,128)} %param.22) | copy-start | bytes 1179652
  208.5 20.1 %copy-start.3 = (f32[3,256]{1,0:T(4,128)}, f32[3,256]{1,0:T(4,128)S(1)}, u32[]{:S(2)}) copy-start(f32[3,256]{1,0:T(4,128)S(1)} %get-tuple-element.163) | copy-start | bytes 9220
Sparse Core Ops, SparseCore 0:
  228.7 56.0 reduce-scatter.3
where the time goes:
time: 293 us
  blocking collectives  152 us (52%)
  other arithmetic  65.7 us (22%)
  waiting for transfers between devices  56.2 us (19%)
  between operations  14.2 us (5%)
    all_gather x6, blocking collectives, local(): lax.all_gather(targets, 'blk', axis=1, tiled=True)  110 us
    unnamed x2, waiting for transfers between devices  56.2 us
    all_gather x1, blocking collectives, local(): all_forces = lax.all_gather(forces, 'blk', axis=2, tiled=True)  24.4 us
    reduce_sum x48, other arithmetic, pair_velocity(): jnp.sum(coef_iso[None] * loads[:, :, None] + (coef_dir * projection)[None...  23.4 us
    reduce_sum x48, other arithmetic, pair_coefs(): dist_sq = jnp.sum(separation * separation, axis=0)  22.6 us
    select_n x48, other arithmetic, pair_coefs(): jnp.where(far_mask, 0.75 * inv_dist * (1.0 + 2.0 / 3.0 * inv_sq), 1.0 - 9...  17.6 us
    all_gather x1, blocking collectives, local(): every_lag = lax.all_gather(lag_index, 'blk', axis=0, tiled=True)  17.5 us
  transfers between devices with their start and end apart: 1, of which 1 were waited for; matrix products, arithmetic and copies ran while one was open for 0% of the time, Pallas kernels for 0%

commit v1 on v0

--- a/solution.py
+++ b/solution.py
@@ -52,7 +52,12 @@
 def local(positions, forces, random_kicks, history_velocity, history_offset, lag_index):
     places = positions
     velocity = jnp.zeros_like(positions)
-    all_forces = lax.all_gather(forces, "blk", axis=2, tiled=True)
+    ring = [forces]
+    for hop in range(15):
+        ring.append(lax.ppermute(ring[-1], "blk", [(dev, (dev + 1) % 16) for dev in range(16)]))
+    all_forces = jnp.roll(
+        jnp.concatenate(ring[::-1], axis=2), (lax.axis_index("blk") + 1) * ring[0].shape[2], axis=2
+    )
     for step_index in range(STEPS):
         targets = places
         step_forces = all_forces[step_index]

time: 293 us -> 350 us (1.19)
  waiting for transfers between devices: 56.2 us -> 134 us
  blocking collectives: 152 us -> 128 us
    ppermute x0 -> x15, waiting for transfers between devices: none -> 78.1 us  [local(): lax.ppermute(ring[-1], 'blk', [(dev, (dev + 1) % 16) for dev in range(16)])]
    all_gather x1 -> x0, blocking collectives: 24.4 us -> none  [local(): all_forces = lax.all_gather(forces, 'blk', axis=2, tiled=True)]
  transfers between devices with their start and end apart: 1 -> 16, of which waited for: 1 -> 14; matrix products, arithmetic and copies ran while one was open for 0% -> 0% of each run, Pallas kernels for 0% -> 0%
where the time goes in v1:
time: 350 us
  waiting for transfers between devices  134 us (38%)
  blocking collectives  128 us (37%)
  other arithmetic  65.7 us (19%)
  between operations  14.4 us (4%)
    all_gather x6, blocking collectives, local(): lax.all_gather(targets, 'blk', axis=1, tiled=True)  110 us
    ppermute x15, waiting for transfers between devices, local(): lax.ppermute(ring[-1], 'blk', [(dev, (dev + 1) % 16) for dev in range(16)])  78.1 us
    unnamed x2, waiting for transfers between devices  56.3 us
    reduce_sum x48, other arithmetic, pair_velocity(): jnp.sum(coef_iso[None] * loads[:, :, None] + (coef_dir * projection)[None...  23.4 us
    reduce_sum x48, other arithmetic, pair_coefs(): dist_sq = jnp.sum(separation * separation, axis=0)  22.6 us
    all_gather x1, blocking collectives, local(): every_lag = lax.all_gather(lag_index, 'blk', axis=0, tiled=True)  18.1 us
    select_n x48, other arithmetic, pair_coefs(): jnp.where(far_mask, 0.75 * inv_dist * (1.0 + 2.0 / 3.0 * inv_sq), 1.0 - 9...  17.6 us
  transfers between devices with their start and end apart: 16, of which 14 were waited for; matrix products, arithmetic and copies ran while one was open for 0% of the time, Pallas kernels for 0%

profile of v1, /device:TPU:0, one launch (start us, length us, event | category | flops | bytes accessed | tf_op | source)
XLA Modules:
  0.0 349.9 jit_solution(2095513304598115798)
XLA Ops:
  7.8 6.7 %collective-permute-done = f32[6,3,256]{2,1,0:T(4,128)S(1)} collective-permute-done((f32[6,3,256]{2,1,0:T(4,128)}, f32[6,3,256]{2,1,0:T(4,128)S(1)}, u32[]{:S(2)}, u32[]{:S(2)}) %collective-permute-start) | collective-permute-done | bytes 18464 | tf_op jit(solution)/shard_map/ppermute | solution.py:57
  14.5 5.9 %collective-permute-done.1 = f32[6,3,256]{2,1,0:T(4,128)S(1)} collective-permute-done((f32[6,3,256]{2,1,0:T(4,128)S(1)}, f32[6,3,256]{2,1,0:T(4,128)S(1)}, u32[]{:S(2)}, u32[]{:S(2)}) %collective-permute-start.1) | collective-permute-done | bytes 18464 | tf_op jit(solution)/shard_map/ppermute | solution.py:57
  20.4 5.9 %collective-permute-done.2 = f32[6,3,256]{2,1,0:T(4,128)S(1)} collective-permute-done((f32[6,3,256]{2,1,0:T(4,128)S(1)}, f32[6,3,256]{2,1,0:T(4,128)S(1)}, u32[]{:S(2)}, u32[]{:S(2)}) %collective-permute-start.2) | collective-permute-done | bytes 18464 | tf_op jit(solution)/shard_map/ppermute | solution.py:57
  26.4 5.9 %collective-permute-done.3 = f32[6,3,256]{2,1,0:T(4,128)S(1)} collective-permute-done((f32[6,3,256]{2,1,0:T(4,128)S(1)}, f32[6,3,256]{2,1,0:T(4,128)S(1)}, u32[]{:S(2)}, u32[]{:S(2)}) %collective-permute-start.3) | collective-permute-done | bytes 18464 | tf_op jit(solution)/shard_map/ppermute | solution.py:57
  32.3 5.9 %collective-permute-done.4 = f32[6,3,256]{2,1,0:T(4,128)S(1)} collective-permute-done((f32[6,3,256]{2,1,0:T(4,128)S(1)}, f32[6,3,256]{2,1,0:T(4,128)S(1)}, u32[]{:S(2)}, u32[]{:S(2)}) %collective-permute-start.4) | collective-permute-done | bytes 18464 | tf_op jit(solution)/shard_map/ppermute | solution.py:57
  38.3 5.9 %collective-permute-done.5 = f32[6,3,256]{2,1,0:T(4,128)S(1)} collective-permute-done((f32[6,3,256]{2,1,0:T(4,128)S(1)}, f32[6,3,256]{2,1,0:T(4,128)S(1)}, u32[]{:S(2)}, u32[]{:S(2)}) %collective-permute-start.5) | collective-permute-done | bytes 18464 | tf_op jit(solution)/shard_map/ppermute | solution.py:57
  44.2 5.9 %collective-permute-done.6 = f32[6,3,256]{2,1,0:T(4,128)S(1)} collective-permute-done((f32[6,3,256]{2,1,0:T(4,128)S(1)}, f32[6,3,256]{2,1,0:T(4,128)S(1)}, u32[]{:S(2)}, u32[]{:S(2)}) %collective-permute-start.6) | collective-permute-done | bytes 18464 | tf_op jit(solution)/shard_map/ppermute | solution.py:57
  50.2 5.9 %collective-permute-done.7 = f32[6,3,256]{2,1,0:T(4,128)S(1)} collective-permute-done((f32[6,3,256]{2,1,0:T(4,128)S(1)}, f32[6,3,256]{2,1,0:T(4,128)S(1)}, u32[]{:S(2)}, u32[]{:S(2)}) %collective-permute-start.7) | collective-permute-done | bytes 18464 | tf_op jit(solution)/shard_map/ppermute | solution.py:57
  56.1 5.9 %collective-permute-done.8 = f32[6,3,256]{2,1,0:T(4,128)S(1)} collective-permute-done((f32[6,3,256]{2,1,0:T(4,128)S(1)}, f32[6,3,256]{2,1,0:T(4,128)S(1)}, u32[]{:S(2)}, u32[]{:S(2)}) %collective-permute-start.8) | collective-permute-done | bytes 18464 | tf_op jit(solution)/shard_map/ppermute | solution.py:57
  62.1 5.9 %collective-permute-done.9 = f32[6,3,256]{2,1,0:T(4,128)S(1)} collective-permute-done((f32[6,3,256]{2,1,0:T(4,128)S(1)}, f32[6,3,256]{2,1,0:T(4,128)S(1)}, u32[]{:S(2)}, u32[]{:S(2)}) %collective-permute-start.9) | collective-permute-done | bytes 18464 | tf_op jit(solution)/shard_map/ppermute | solution.py:57
  68.0 5.9 %collective-permute-done.10 = f32[6,3,256]{2,1,0:T(4,128)S(1)} collective-permute-done((f32[6,3,256]{2,1,0:T(4,128)S(1)}, f32[6,3,256]{2,1,0:T(4,128)S(1)}, u32[]{:S(2)}, u32[]{:S(2)}) %collective-permute-start.10) | collective-permute-done | bytes 18464 | tf_op jit(solution)/shard_map/ppermute | solution.py:57
  74.0 5.9 %collective-permute-done.11 = f32[6,3,256]{2,1,0:T(4,128)S(1)} collective-permute-done((f32[6,3,256]{2,1,0:T(4,128)S(1)}, f32[6,3,256]{2,1,0:T(4,128)S(1)}, u32[]{:S(2)}, u32[]{:S(2)}) %collective-permute-start.11) | collective-permute-done | bytes 18464 | tf_op jit(solution)/shard_map/ppermute | solution.py:57
  79.9 5.9 %collective-permute-done.12 = f32[6,3,256]{2,1,0:T(4,128)S(1)} collective-permute-done((f32[6,3,256]{2,1,0:T(4,128)S(1)}, f32[6,3,256]{2,1,0:T(4,128)S(1)}, u32[]{:S(2)}, u32[]{:S(2)}) %collective-permute-start.12) | collective-permute-done | bytes 18464 | tf_op jit(solution)/shard_map/ppermute | solution.py:57
  85.9 18.1 %all-gather = s32[16,1,128]{2,1,0:T(1,128)S(1)} all-gather(s32[1,1,128]{2,1,0:T(1,128)} %bitcast.108), channel_id=1, replica_groups=mesh['rep'=2,'blk'=16] {'blk'}, dimensions={0}, use_global_device_ids=true | all-gather | bytes 8704 | tf_op jit(solution)/shard_map/all_gather | solution.py:73
  104.2 18.9 %all_gather.21 = f32[3,4096]{1,0:T(4,128)S(1)} all-gather(f32[3,256]{1,0:T(4,128)} %param.18), channel_id=1, replica_groups=mesh['rep'=2,'blk'=16] {'blk'}, dimensions={1}, use_global_device_ids=true | all-gather | bytes 52224 | tf_op jit(solution)/shard_map/all_gather | solution.py:65
  123.3 0.8 constant_dynamic-update-slice_fusion.16
  124.5 11.2 %while.66 = (s32[]{:T(128)}, f32[3,256]{1,0:T(4,128)S(1)}, f32[3,256]{1,0:T(4,128)S(1)}, f32[8,3,512]{2,1,0:T(4,128)S(1)}, f32[8,3,512]{2,1,0:T(4,128)S(1)}, /*index=5*/s32[]{:T(128)}, s32[]{:T(128)}) while((s32[]{:T(128)}, f32[3,256]{1,0:T(4,128)S(1)}, f32[3,256]{1,0:T(4,128)S(1)}, f32[8,3,512]{2,1,0:T(4,128)S(1)}, ...), condition=%wide.region_4.5_spmd.clone, body=%wide.region_0.4_spmd.clone.sunk | while | flops 6161155 | bytes 4261979 | solution.py:46
  135.7 17.9 %all_gather.22 = f32[3,4096]{1,0:T(4,128)S(1)} all-gather(f32[3,256]{1,0:T(4,128)S(1)} %bitcast_add_fusion.5), channel_id=1, replica_groups=mesh['rep'=2,'blk'=16] {'blk'}, dimensions={1}, use_global_device_ids=true | all-gather | bytes 52224 | tf_op jit(solution)/shard_map/all_gather | solution.py:65
  153.6 11.2 %while.67 = (s32[]{:T(128)}, f32[3,256]{1,0:T(4,128)S(1)}, f32[3,256]{1,0:T(4,128)S(1)}, f32[8,3,512]{2,1,0:T(4,128)S(1)}, f32[8,3,512]{2,1,0:T(4,128)S(1)}, /*index=5*/s32[]{:T(128)}, s32[]{:T(128)}) while((s32[]{:T(128)}, f32[3,256]{1,0:T(4,128)S(1)}, f32[3,256]{1,0:T(4,128)S(1)}, f32[8,3,512]{2,1,0:T(4,128)S(1)}, ...), condition=%wide.region_9.10_spmd.clone, body=%wide.region_5.9_spmd.clone.sunk | while | flops 6161155 | bytes 4261979 | solution.py:46
  164.8 18.7 %all_gather.23 = f32[3,4096]{1,0:T(4,128)S(1)} all-gather(f32[3,256]{1,0:T(4,128)S(1)} %bitcast_add_fusion.4), channel_id=1, replica_groups=mesh['rep'=2,'blk'=16] {'blk'}, dimensions={1}, use_global_device_ids=true | all-gather | bytes 52224 | tf_op jit(solution)/shard_map/all_gather | solution.py:65
  183.4 11.2 %while.68 = (s32[]{:T(128)}, f32[3,256]{1,0:T(4,128)S(1)}, f32[3,256]{1,0:T(4,128)S(1)}, f32[8,3,512]{2,1,0:T(4,128)S(1)}, f32[8,3,512]{2,1,0:T(4,128)S(1)}, /*index=5*/s32[]{:T(128)}, s32[]{:T(128)}) while((s32[]{:T(128)}, f32[3,256]{1,0:T(4,128)S(1)}, f32[3,256]{1,0:T(4,128)S(1)}, f32[8,3,512]{2,1,0:T(4,128)S(1)}, ...), condition=%wide.region_14.15_spmd.clone, body=%wide.region_10.14_spmd.clone.sunk | while | flops 6161155 | bytes 4261979 | solution.py:46
  194.6 17.9 %all_gather.24 = f32[3,4096]{1,0:T(4,128)S(1)} all-gather(f32[3,256]{1,0:T(4,128)S(1)} %bitcast_add_fusion.3), channel_id=1, replica_groups=mesh['rep'=2,'blk'=16] {'blk'}, dimensions={1}, use_global_device_ids=true | all-gather | bytes 52224 | tf_op jit(solution)/shard_map/all_gather | solution.py:65
  212.5 11.2 %while.69 = (s32[]{:T(128)}, f32[3,256]{1,0:T(4,128)S(1)}, f32[3,256]{1,0:T(4,128)S(1)}, f32[8,3,512]{2,1,0:T(4,128)S(1)}, f32[8,3,512]{2,1,0:T(4,128)S(1)}, /*index=5*/s32[]{:T(128)}, s32[]{:T(128)}) while((s32[]{:T(128)}, f32[3,256]{1,0:T(4,128)S(1)}, f32[3,256]{1,0:T(4,128)S(1)}, f32[8,3,512]{2,1,0:T(4,128)S(1)}, ...), condition=%wide.region_19.20_spmd.clone, body=%wide.region_15.19_spmd.clone.sunk | while | flops 6161155 | bytes 4261979 | solution.py:46
  223.7 18.7 %all_gather.25 = f32[3,4096]{1,0:T(4,128)S(1)} all-gather(f32[3,256]{1,0:T(4,128)S(1)} %bitcast_add_fusion.2), channel_id=1, replica_groups=mesh['rep'=2,'blk'=16] {'blk'}, dimensions={1}, use_global_device_ids=true | all-gather | bytes 52224 | tf_op jit(solution)/shard_map/all_gather | solution.py:65
  242.3 11.1 %while.70 = (s32[]{:T(128)}, f32[3,256]{1,0:T(4,128)S(1)}, f32[3,256]{1,0:T(4,128)S(1)}, f32[8,3,512]{2,1,0:T(4,128)S(1)}, f32[8,3,512]{2,1,0:T(4,128)S(1)}, /*index=5*/s32[]{:T(128)}, s32[]{:T(128)}) while((s32[]{:T(128)}, f32[3,256]{1,0:T(4,128)S(1)}, f32[3,256]{1,0:T(4,128)S(1)}, f32[8,3,512]{2,1,0:T(4,128)S(1)}, ...), condition=%wide.region_24.25_spmd.clone, body=%wide.region_20.24_spmd.clone.sunk | while | flops 6161155 | bytes 4261979 | solution.py:46
  253.5 18.1 %all_gather.26 = f32[3,4096]{1,0:T(4,128)S(1)} all-gather(f32[3,256]{1,0:T(4,128)S(1)} %bitcast_add_fusion.1), channel_id=1, replica_groups=mesh['rep'=2,'blk'=16] {'blk'}, dimensions={1}, use_global_device_ids=true | all-gather | bytes 52224 | tf_op jit(solution)/shard_map/all_gather | solution.py:65
  271.6 11.2 %while.71 = (s32[]{:T(128)}, f32[3,256]{1,0:T(4,128)S(1)}, f32[3,256]{1,0:T(4,128)S(1)}, f32[8,3,512]{2,1,0:T(4,128)S(1)}, f32[8,3,512]{2,1,0:T(4,128)S(1)}, /*index=5*/s32[]{:T(128)}, s32[]{:T(128)}) while((s32[]{:T(128)}, f32[3,256]{1,0:T(4,128)S(1)}, f32[3,256]{1,0:T(4,128)S(1)}, f32[8,3,512]{2,1,0:T(4,128)S(1)}, ...), condition=%wide.region_29.30_spmd.clone, body=%wide.region_25.29_spmd.clone.sunk | while | flops 6161155 | bytes 4261979 | solution.py:46
  282.7 0.6 fusion.53
  283.6 1.7 convolution_bitcast_fusion
  285.4 56.3 %reduce-scatter.4.cloned.1.call-done = f32[128,2]{1,0:T(8,128)} async-done(((f32[2048,2]{1,0:T(8,128)}), f32[128,2]{1,0:T(8,128)}) %reduce-scatter.4.cloned.1.call-update) | async-done | bytes 1040
  341.6 0.9 copy.25
  342.5 0.6 broadcast_multiply_fusion
  (316 shorter events, 66.3 us)
Async XLA Ops:
  7.2 117.2 %copy-start.4 = (f32[6,3,256]{2,1,0:T(4,128)S(1)}, f32[6,3,256]{2,1,0:T(4,128)}, u32[]{:S(2)}) copy-start(f32[6,3,256]{2,1,0:T(4,128)} %param.19) | copy-start | bytes 55300
  7.2 334.4 %reduce-scatter.4.cloned.1.call-start = ((), (), s32[]{:S(2)}) async-start(), calls=%async_computation.1 | async-start | bytes 1114112
  7.2 7.2 %collective-permute-start = (f32[6,3,256]{2,1,0:T(4,128)}, f32[6,3,256]{2,1,0:T(4,128)S(1)}, u32[]{:S(2)}, u32[]{:S(2)}) collective-permute-start(f32[6,3,256]{2,1,0:T(4,128)} %param.19), channel_id=1, source_target_pairs={{0,1},{1,2},{2,3},{3,4},{4,5},{5,6},{6,7},{7,8},{8,9},{9,10},{10,1... | collective-permute-start | bytes 55304 | tf_op jit(solution)/shard_map/ppermute | solution.py:57
  14.5 5.9 %collective-permute-start.1 = (f32[6,3,256]{2,1,0:T(4,128)S(1)}, f32[6,3,256]{2,1,0:T(4,128)S(1)}, u32[]{:S(2)}, u32[]{:S(2)}) collective-permute-start(f32[6,3,256]{2,1,0:T(4,128)S(1)} %collective-permute-done), channel_id=1, source_target_pairs={{0,1},{1,2},{2,3},{3,4},{4,5},{5,6},{6,7},{7,8},{8,9},{9,10},{10,1... | collective-permute-start | bytes 55304 | tf_op jit(solution)/shard_map/ppermute | solution.py:57
  20.4 5.9 %collective-permute-start.2 = (f32[6,3,256]{2,1,0:T(4,128)S(1)}, f32[6,3,256]{2,1,0:T(4,128)S(1)}, u32[]{:S(2)}, u32[]{:S(2)}) collective-permute-start(f32[6,3,256]{2,1,0:T(4,128)S(1)} %collective-permute-done.1), channel_id=1, source_target_pairs={{0,1},{1,2},{2,3},{3,4},{4,5},{5,6},{6,7},{7,8},{8,9},{9,10},{10,1... | collective-permute-start | bytes 55304 | tf_op jit(solution)/shard_map/ppermute | solution.py:57
  26.4 5.9 %collective-permute-start.3 = (f32[6,3,256]{2,1,0:T(4,128)S(1)}, f32[6,3,256]{2,1,0:T(4,128)S(1)}, u32[]{:S(2)}, u32[]{:S(2)}) collective-permute-start(f32[6,3,256]{2,1,0:T(4,128)S(1)} %collective-permute-done.2), channel_id=1, source_target_pairs={{0,1},{1,2},{2,3},{3,4},{4,5},{5,6},{6,7},{7,8},{8,9},{9,10},{10,1... | collective-permute-start | bytes 55304 | tf_op jit(solution)/shard_map/ppermute | solution.py:57
  32.3 5.9 %collective-permute-start.4 = (f32[6,3,256]{2,1,0:T(4,128)S(1)}, f32[6,3,256]{2,1,0:T(4,128)S(1)}, u32[]{:S(2)}, u32[]{:S(2)}) collective-permute-start(f32[6,3,256]{2,1,0:T(4,128)S(1)} %collective-permute-done.3), channel_id=1, source_target_pairs={{0,1},{1,2},{2,3},{3,4},{4,5},{5,6},{6,7},{7,8},{8,9},{9,10},{10,1... | collective-permute-start | bytes 55304 | tf_op jit(solution)/shard_map/ppermute | solution.py:57
  38.3 5.9 %collective-permute-start.5 = (f32[6,3,256]{2,1,0:T(4,128)S(1)}, f32[6,3,256]{2,1,0:T(4,128)S(1)}, u32[]{:S(2)}, u32[]{:S(2)}) collective-permute-start(f32[6,3,256]{2,1,0:T(4,128)S(1)} %collective-permute-done.4), channel_id=1, source_target_pairs={{0,1},{1,2},{2,3},{3,4},{4,5},{5,6},{6,7},{7,8},{8,9},{9,10},{10,1... | collective-permute-start | bytes 55304 | tf_op jit(solution)/shard_map/ppermute | solution.py:57
  44.2 5.9 %collective-permute-start.6 = (f32[6,3,256]{2,1,0:T(4,128)S(1)}, f32[6,3,256]{2,1,0:T(4,128)S(1)}, u32[]{:S(2)}, u32[]{:S(2)}) collective-permute-start(f32[6,3,256]{2,1,0:T(4,128)S(1)} %collective-permute-done.5), channel_id=1, source_target_pairs={{0,1},{1,2},{2,3},{3,4},{4,5},{5,6},{6,7},{7,8},{8,9},{9,10},{10,1... | collective-permute-start | bytes 55304 | tf_op jit(solution)/shard_map/ppermute | solution.py:57
  50.2 5.9 %collective-permute-start.7 = (f32[6,3,256]{2,1,0:T(4,128)S(1)}, f32[6,3,256]{2,1,0:T(4,128)S(1)}, u32[]{:S(2)}, u32[]{:S(2)}) collective-permute-start(f32[6,3,256]{2,1,0:T(4,128)S(1)} %collective-permute-done.6), channel_id=1, source_target_pairs={{0,1},{1,2},{2,3},{3,4},{4,5},{5,6},{6,7},{7,8},{8,9},{9,10},{10,1... | collective-permute-start | bytes 55304 | tf_op jit(solution)/shard_map/ppermute | solution.py:57
  56.1 5.9 %collective-permute-start.8 = (f32[6,3,256]{2,1,0:T(4,128)S(1)}, f32[6,3,256]{2,1,0:T(4,128)S(1)}, u32[]{:S(2)}, u32[]{:S(2)}) collective-permute-start(f32[6,3,256]{2,1,0:T(4,128)S(1)} %collective-permute-done.7), channel_id=1, source_target_pairs={{0,1},{1,2},{2,3},{3,4},{4,5},{5,6},{6,7},{7,8},{8,9},{9,10},{10,1... | collective-permute-start | bytes 55304 | tf_op jit(solution)/shard_map/ppermute | solution.py:57
  62.1 5.9 %collective-permute-start.9 = (f32[6,3,256]{2,1,0:T(4,128)S(1)}, f32[6,3,256]{2,1,0:T(4,128)S(1)}, u32[]{:S(2)}, u32[]{:S(2)}) collective-permute-start(f32[6,3,256]{2,1,0:T(4,128)S(1)} %collective-permute-done.8), channel_id=1, source_target_pairs={{0,1},{1,2},{2,3},{3,4},{4,5},{5,6},{6,7},{7,8},{8,9},{9,10},{10,1... | collective-permute-start | bytes 55304 | tf_op jit(solution)/shard_map/ppermute | solution.py:57
  68.0 5.9 %collective-permute-start.10 = (f32[6,3,256]{2,1,0:T(4,128)S(1)}, f32[6,3,256]{2,1,0:T(4,128)S(1)}, u32[]{:S(2)}, u32[]{:S(2)}) collective-permute-start(f32[6,3,256]{2,1,0:T(4,128)S(1)} %collective-permute-done.9), channel_id=1, source_target_pairs={{0,1},{1,2},{2,3},{3,4},{4,5},{5,6},{6,7},{7,8},{8,9},{9,10},{10,1... | collective-permute-start | bytes 55304 | tf_op jit(solution)/shard_map/ppermute | solution.py:57
  74.0 5.9 %collective-permute-start.11 = (f32[6,3,256]{2,1,0:T(4,128)S(1)}, f32[6,3,256]{2,1,0:T(4,128)S(1)}, u32[]{:S(2)}, u32[]{:S(2)}) collective-permute-start(f32[6,3,256]{2,1,0:T(4,128)S(1)} %collective-permute-done.10), channel_id=1, source_target_pairs={{0,1},{1,2},{2,3},{3,4},{4,5},{5,6},{6,7},{7,8},{8,9},{9,10},{10,1... | collective-permute-start | bytes 55304 | tf_op jit(solution)/shard_map/ppermute | solution.py:57
  79.9 5.9 %collective-permute-start.12 = (f32[6,3,256]{2,1,0:T(4,128)S(1)}, f32[6,3,256]{2,1,0:T(4,128)S(1)}, u32[]{:S(2)}, u32[]{:S(2)}) collective-permute-start(f32[6,3,256]{2,1,0:T(4,128)S(1)} %collective-permute-done.11), channel_id=1, source_target_pairs={{0,1},{1,2},{2,3},{3,4},{4,5},{5,6},{6,7},{7,8},{8,9},{9,10},{10,1... | collective-permute-start | bytes 55304 | tf_op jit(solution)/shard_map/ppermute | solution.py:57
  85.9 18.2 %collective-permute-start.13 = (f32[6,3,256]{2,1,0:T(4,128)S(1)}, f32[6,3,256]{2,1,0:T(4,128)S(1)}, u32[]{:S(2)}, u32[]{:S(2)}) collective-permute-start(f32[6,3,256]{2,1,0:T(4,128)S(1)} %collective-permute-done.12), channel_id=1, source_target_pairs={{0,1},{1,2},{2,3},{3,4},{4,5},{5,6},{6,7},{7,8},{8,9},{9,10},{10,1... | collective-permute-start | bytes 55304 | tf_op jit(solution)/shard_map/ppermute | solution.py:57
  104.0 19.0 %collective-permute-start.14 = (f32[6,3,256]{2,1,0:T(4,128)S(1)}, f32[6,3,256]{2,1,0:T(4,128)S(1)}, u32[]{:S(2)}, u32[]{:S(2)}) collective-permute-start(f32[6,3,256]{2,1,0:T(4,128)S(1)} %collective-permute-done.13), channel_id=1, source_target_pairs={{0,1},{1,2},{2,3},{3,4},{4,5},{5,6},{6,7},{7,8},{8,9},{9,10},{10,1... | collective-permute-start | bytes 55304 | tf_op jit(solution)/shard_map/ppermute | solution.py:57
  123.2 1.3 copy-start
  124.5 11.2 %copy-start.5 = (f32[6,3,256]{2,1,0:T(4,128)S(1)}, f32[6,3,256]{2,1,0:T(4,128)}, u32[]{:S(2)}) copy-start(f32[6,3,256]{2,1,0:T(4,128)} %param.20) | copy-start | bytes 55300
  271.6 11.8 %copy-start.1 = (f32[128,3,256]{2,0,1:T(8,128)S(1)}, f32[128,3,256]{2,0,1:T(8,128)}, u32[]{:S(2)}) copy-start(f32[128,3,256]{2,0,1:T(8,128)} %param.21) | copy-start | bytes 1179652
  271.6 11.9 %copy-start.2 = (f32[128,3,256]{2,0,1:T(8,128)S(1)}, f32[128,3,256]{2,0,1:T(8,128)}, u32[]{:S(2)}) copy-start(f32[128,3,256]{2,0,1:T(8,128)} %param.22) | copy-start | bytes 1179652
  282.7 2.6 copy-start.3
Sparse Core Ops, SparseCore 0:
  285.5 56.0 reduce-scatter.3
